TPU v7x, 32 devices: a whole 2x2x4 slice. The times are simulated.
32 devices in a mesh: chain: 4 (over y, core), cols: 8 (over z, x).
Axes of the slice: x: 2, y: 2, z: 4, core: 2. Of those that a mesh axis runs over, the one named last changes fastest.
Arguments:
- factor: float32 [4608, 4608], P(('chain', 'cols')), may hold values from -2 to 2, as said below
- right_side: float32 [4608, 1024], P('chain', 'cols'), may hold values from -6 to 6
- occ_order: int32 [16], replicated, may hold values from 0 to 15, each once
- cabs_order: int32 [64], replicated, may hold values from 0 to 63, each once
Outputs:
- fitted: float32 [16, 64, 4608], P('cols', None, 'chain')
Inputs may be any that keep to these rules, and one draw needn't show every extreme that they name: factor is lower triangular: zero above the diagonal, its diagonal between 1 and 2.
All inputs are finite; a program needn't handle non-finite values.
Results may differ from a plain program's by a relative error of at most 0.00017.
Values sent between devices are 32-bit elements; how exact they have to be, the bound alone decides.
A program may use at most 128 MiB of HBM per device.

v0:
```python
import jax
import jax.numpy as jnp
from jax import lax
from jax.sharding import PartitionSpec as P


def from_root(value, axis, source):
    kept = jnp.where(lax.axis_index(axis) == source, value, 0).astype(value.dtype)
    return lax.psum(kept, axis)


def product(left, right):
    return jnp.dot(left, right, precision=lax.Precision.HIGHEST, preferred_element_type=jnp.float32)


def per_device(factor, right_side, occ_order, cabs_order):
    chain_size = lax.axis_size("chain")
    position = lax.axis_index("chain")
    factor_row = lax.all_gather(factor, "cols", axis=0, tiled=True)
    aux_rows = factor_row.shape[0]
    diag_block = lax.dynamic_slice_in_dim(factor_row, position * aux_rows, aux_rows, 1)
    identity = jnp.eye(aux_rows, dtype=jnp.float32)
    inverse = jax.scipy.linalg.solve_triangular(diag_block, identity, lower=True)

    def settle(residual):
        return product(inverse, residual)

    def blank(residual):
        return jnp.zeros_like(residual)

    residual = right_side
    solution = jnp.zeros_like(right_side)
    for section in range(chain_size):
        solved = lax.cond(position == section, settle, blank, residual)
        solution = solution + solved
        if section + 1 < chain_size:
            arrived = from_root(solved, "chain", section)
            coupling = factor_row[:, section * aux_rows : (section + 1) * aux_rows]

            def lower_block(current, arrived=arrived, coupling=coupling):
                return current - product(coupling, arrived)

            def keep_block(current):
                return current

            residual = lax.cond(position > section, lower_block, keep_block, residual)
    occ_total = occ_order.shape[0]
    cabs_local = right_side.shape[1] // occ_total
    cols_size = lax.axis_size("cols")
    occ_local = occ_total // cols_size
    grid = solution.reshape(aux_rows, cabs_local, occ_total)
    grid = jnp.take(grid, occ_order, axis=2)
    grid = grid.reshape(aux_rows, cabs_local, cols_size, occ_local)
    grid = jnp.transpose(grid, (2, 3, 1, 0))
    moved = jnp.take(
        lax.all_to_all(grid, "cols", split_axis=0, concat_axis=2, tiled=True), cabs_order, axis=2
    )
    return moved.reshape(occ_local, moved.shape[2], aux_rows)


def solution(mesh):
    in_specs = (P(("chain", "cols"), None), P("chain", "cols"), P(), P())
    out_specs = P("cols", None, "chain")
    return jax.shard_map(
        per_device, mesh=mesh, in_specs=in_specs, out_specs=out_specs, check_vma=False
    )
```

profile of v0, /device:TPU:5, one launch (start us, length us, event | category | flops | bytes accessed | tf_op | source)
XLA Modules:
  0.0 739.5 jit_solution(7682201106156119193)
XLA Ops:
  6.5 1.1 copy.72
  7.7 0.4 iota_compare_fusion
  8.1 2.7 fusion.27
  10.8 405.7 %all-gather.2.cloned.1.call-done = f32[1152,4608]{1,0:T(8,128)} async-done(((f32[144,4608]{1,0:T(8,128)}), f32[1152,4608]{1,0:T(8,128)}) %all-gather.2.cloned.1.call-update) | async-done | bytes 21233680 | tf_op jit(solution)/shard_map/all_gather | solution.py:19
  416.6 5.2 dynamic-slice_select_fusion
  421.8 25.2 %while.1 = (s32[]{:T(128)}, f32[1152,1152]{1,0:T(8,128)}, s32[9,2]{0,1:T(2,128)S(1)}, f32[9,128,128]{2,1,0:T(8,128)S(1)}, s32[]{:T(128)}) while((s32[]{:T(128)}, f32[1152,1152]{1,0:T(8,128)}, s32[9,2]{0,1:T(2,128)S(1)}, f32[9,128,128]{2,1,0:T(8,128)S(1)}, s32[]{:T(128)}) %tuple.105), condition=%wide.while_cond, body=%wide.while_body.sunk | while | flops 2 | bytes 131181 | solution.py:23
  421.8 0.5 fusion.82
  422.4 2.2 bitcast_dynamic-update-slice_fusion.2
  424.6 0.5 fusion.82
  425.2 2.2 bitcast_dynamic-update-slice_fusion.2
  427.5 0.5 fusion.82
  428.0 2.2 bitcast_dynamic-update-slice_fusion.2
  430.3 0.5 fusion.82
  430.8 2.2 bitcast_dynamic-update-slice_fusion.2
  433.1 0.5 fusion.82
  433.6 2.2 bitcast_dynamic-update-slice_fusion.2
  435.9 0.5 fusion.82
  436.4 2.2 bitcast_dynamic-update-slice_fusion.2
  438.7 0.5 fusion.82
  439.2 2.2 bitcast_dynamic-update-slice_fusion.2
  441.5 0.5 fusion.82
  442.1 2.2 bitcast_dynamic-update-slice_fusion.2
  444.3 0.5 fusion.82
  444.9 2.1 bitcast_dynamic-update-slice_fusion.2
  447.0 88.9 %custom-call.4 = f32[9,128,128]{1,2,0:T(8,128)S(1)} custom-call(f32[9,128,128]{2,1,0:T(8,128)S(1)} %get-tuple-element.90), custom_call_target="InvertDiagBlocksLowerTriangular" | custom-call | tf_op jit(solution)/shard_map/jit(_solve_triangular)/triangular_solve | solution.py:23
  535.9 0.7 constant_dynamic-update-slice_fusion.25
  536.6 2.1 convolution_subtract_fusion.7
  538.7 0.9 constant_dynamic-update-slice_fusion.24
  539.6 1.7 convolution_subtract_fusion.6
  541.3 0.8 constant_dynamic-update-slice_fusion.23
  542.1 2.3 convolution_subtract_fusion.2
  544.4 0.9 constant_dynamic-update-slice_fusion.22
  545.3 2.4 convolution_subtract_fusion.5
  547.7 0.8 constant_dynamic-update-slice_fusion.21
  548.5 3.0 convolution_subtract_fusion
  551.5 0.7 constant_dynamic-update-slice_fusion.20
  552.2 3.4 convolution_subtract_fusion.1
  555.6 0.7 constant_dynamic-update-slice_fusion.19
  556.3 3.7 convolution_subtract_fusion.4
  560.0 0.7 constant_dynamic-update-slice_fusion.18
  560.7 3.9 convolution_subtract_fusion.3
  564.6 0.7 convolution_dynamic-update-slice_fusion
  565.3 2.3 copy-done
  567.9 0.9 broadcast_select_fusion.2
  568.8 35.9 %all-reduce.4.cloned.1.call-done = f32[1152,128]{1,0:T(8,128)} async-done(((f32[1152,128]{1,0:T(8,128)}), f32[1152,128]{1,0:T(8,128)}) %all-reduce.4.cloned.1.call-update) | async-done | bytes 589840 | tf_op jit(solution)/shard_map/psum | solution.py:9
  604.7 6.4 conditional.8
  604.7 6.4 fusion.2
  611.2 0.9 broadcast_select_fusion.1
  612.3 38.6 %all-reduce.6.cloned.1.call-done = f32[1152,128]{1,0:T(8,128)} async-done(((f32[1152,128]{1,0:T(8,128)}), f32[1152,128]{1,0:T(8,128)}) %all-reduce.6.cloned.1.call-update) | async-done | bytes 589840 | tf_op jit(solution)/shard_map/psum | solution.py:9
  650.9 6.4 conditional.10
  650.9 6.4 fusion.7
  657.4 0.9 broadcast_select_fusion
  659.0 39.4 %all-reduce.8.cloned.1.call-done = f32[1152,128]{1,0:T(8,128)} async-done(((f32[1152,128]{1,0:T(8,128)}), f32[1152,128]{1,0:T(8,128)}) %all-reduce.8.cloned.1.call-update) | async-done | bytes 589840 | tf_op jit(solution)/shard_map/psum | solution.py:9
  698.4 6.7 conditional.12
  698.6 6.4 fusion.12
  705.0 7.4 %conditional.13 = (f32[1152,128]{0,1:T(8,128)S(1)}) conditional(s32[]{:T(128)} %convert_element_type.48, () %tuple.55, (f32[1152,1152]{1,0:T(8,128)}, f32[1152,128]{1,0:T(8,128)S(1)}) %tuple.132), branch_computations={%region_15.16_spmd, %region_16.17_spmd} | conditional | flops 2038431744 | bytes 6488072 | solution.py:34
  705.0 7.4 %fusion.55 = f32[1152,128]{0,1:T(8,128)S(1)} fusion(f32[1152,1152]{1,0:T(8,128)} %get-tuple-element.79, f32[1152,128]{1,0:T(8,128)S(1)} %get-tuple-element.80), kind=kOutput, calls=%fused_computation.122 | convolution fusion | flops 2038431744 | bytes 6488064 | tf_op jit(solution)/shard_map/cond | solution.py:34
  712.8 0.6 gather_fusion
  713.4 0.9 select_bitcast_fusion.1
  714.3 5.5 all-to-all-start
  719.8 9.8 %all-to-all-done = f32[8,2,8,1152]{3,2,1,0:T(8,128)S(1)} async-done(((f32[8,2,8,1152]{3,2,1,0:T(8,128)}), f32[8,2,8,1152]{3,2,1,0:T(8,128)S(1)}, u32[]{:S(2)}, u32[]{:S(2)}) %all-to-all-start) | async-done | bytes 589856 | tf_op jit(solution)/shard_map/all_to_all | solution.py:56
  729.7 0.5 copy.11
  730.2 1.2 gather_fusion.1
  731.7 0.9 copy.12
  (46 shorter events, 2.9 us)
Async XLA Ops:
  6.5 410.0 %all-gather.2.cloned.1.call-start = ((), (), s32[]{:S(2)}) async-start(), calls=%async_computation.1 | async-start | bytes 23887872 | tf_op jit(solution)/shard_map/all_gather | solution.py:19
  7.6 597.1 %all-reduce.4.cloned.1.call-start = ((), (), s32[]{:S(2)}) async-start(), calls=%async_computation.2 | async-start | bytes 1179648 | tf_op jit(solution)/shard_map/psum | solution.py:9
  535.9 3.6 copy-start.1
  565.3 2.3 copy-start
  568.8 82.1 %all-reduce.6.cloned.1.call-start = ((), (), s32[]{:S(2)}) async-start(), calls=%async_computation.3 | async-start | bytes 1179648 | tf_op jit(solution)/shard_map/psum | solution.py:9
  611.1 1.0 copy-start.2
  612.1 86.2 %all-reduce.8.cloned.1.call-start = ((), (), s32[]{:S(2)}) async-start(), calls=%async_computation.4 | async-start | bytes 1179648 | tf_op jit(solution)/shard_map/psum | solution.py:9
  657.3 1.0 copy-start.3
  714.3 15.3 %all-to-all-start = ((f32[8,2,8,1152]{3,2,1,0:T(8,128)}), f32[8,2,8,1152]{3,2,1,0:T(8,128)S(1)}, u32[]{:S(2)}, u32[]{:S(2)}) async-start(f32[8,2,8,1152]{3,2,1,0:T(8,128)} %select_bitcast_fusion.1), calls=%async_computation | async-start | bytes 1179648 | tf_op jit(solution)/shard_map/all_to_all | solution.py:56
Sparse Core Ops, SparseCore 0:
  8.9 407.6 all-gather.1
  568.9 35.8 all-reduce.3
  612.2 38.5 all-reduce.5
  658.4 39.9 all-reduce.7
where the time goes:
time: 743 us; the launch traced here: 740 us
  waiting for transfers between devices  529 us (71%)
  other arithmetic  101 us (14%)
  matrix products  55.8 us (8%)
  local copies, waits for them, and re-layouts  32.7 us (4%)
  between operations  13.9 us (2%)
    all_gather x1, waiting for transfers between devices, per_device(): factor_row = lax.all_gather(factor, 'cols', axis=0, tiled=True)  406 us
    psum x3, waiting for transfers between devices, from_root(): return lax.psum(kept, axis)  114 us
    another operation x3, other arithmetic, per_device(): jax.scipy.linalg.solve_triangular(diag_block, identity, lower=True)  94.1 us
    another operation x17, matrix products, per_device(): jax.scipy.linalg.solve_triangular(diag_block, identity, lower=True)  29.2 us
    another operation x30, local copies, waits for them, and re-layouts  25.2 us
    dot_general x3, matrix products, product(): jnp.dot(left, right, precision=lax.Precision.HIGHEST, preferred_element_t...  19.2 us
  transfers between devices with their start and end apart: 5, of which 5 were waited for; matrix products, arithmetic and copies ran while one was open for 1% of the time, Pallas kernels for 0%

commit v1 on v0

--- a/solution.py
+++ b/solution.py
@@ -1,7 +1,15 @@
+import functools
+
 import jax
 import jax.numpy as jnp
 from jax import lax
+from jax.experimental import pallas as pl
+from jax.experimental.pallas import tpu as pltpu
 from jax.sharding import PartitionSpec as P
+
+BLOCK = 128
+PIECE = 8
+MESH = pl.DeviceIdType.MESH
 
 
 def from_root(value, axis, source):
@@ -13,7 +21,7 @@
     return jnp.dot(left, right, precision=lax.Precision.HIGHEST, preferred_element_type=jnp.float32)
 
 
-def per_device(factor, right_side, occ_order, cabs_order):
+def general(factor, right_side, occ_order, cabs_order):
     chain_size = lax.axis_size("chain")
     position = lax.axis_index("chain")
     factor_row = lax.all_gather(factor, "cols", axis=0, tiled=True)
@@ -58,7 +66,275 @@
     return moved.reshape(occ_local, moved.shape[2], aux_rows)
 
 
+def times_t(left, right, exact=False):
+    precision = lax.Precision.HIGHEST
+    dims = (((1,), (1,)), ((), ()))
+    if exact:
+        return lax.dot_general(left, right, dims, precision=precision, preferred_element_type=jnp.float32)
+    left_hi = left.astype(jnp.bfloat16)
+    left_lo = (left - left_hi.astype(jnp.float32)).astype(jnp.bfloat16)
+    right_hi = right.astype(jnp.bfloat16)
+    right_lo = (right - right_hi.astype(jnp.float32)).astype(jnp.bfloat16)
+    dot = functools.partial(lax.dot_general, dimension_numbers=dims, preferred_element_type=jnp.float32)
+    return dot(left_hi, right_hi) + (dot(left_hi, right_lo) + dot(left_lo, right_hi))
+
+
+def plain(left, right):
+    return jnp.dot(left, right, precision=lax.Precision.HIGHEST, preferred_element_type=jnp.float32)
+
+
+def kernel(
+    chains, ring, strip_ref, rhs_ref, out_ref, rows, resid, solved, inverse,
+    send, recv, chain_send, chain_recv, rhs_send, rhs_recv, local_sem,
+):
+    cols = 2 * ring
+    strip = strip_ref.shape[0]
+    aux = strip * cols
+    blocks = aux // BLOCK
+    cabs_local = rhs_ref.shape[2]
+    width = out_ref.shape[0] * out_ref.shape[1]
+    me = lax.axis_index("chain")
+    k = lax.axis_index("cols")
+    z = k // 2
+    x = k % 2
+    up, down, far = (z + 1) % ring, (z + ring - 1) % ring, (z + 2) % ring
+    partner = 2 * z + (1 - x)
+    above, below = 2 * up + x, 2 * down + x
+
+    units = strip // PIECE
+    near_half = (units * 5 // 9 // 2) * PIECE
+    near = 2 * near_half
+    far_half = (strip - near) // 2
+    tail = near + far_half
+
+    def slot(zz, xx, begin, size, q):
+        start = pl.multiple_of((2 * zz + xx) * strip + begin, PIECE)
+        column = me if q == 0 else q - 1
+        return rows.at[pl.ds(start, size), pl.ds(pl.multiple_of(column * aux, BLOCK), aux)]
+
+    def push(q, i, zz, xx, begin, size, to):
+        ref = slot(zz, xx, begin, size, q)
+        return pltpu.make_async_remote_copy(
+            src_ref=ref, dst_ref=ref, send_sem=send.at[q, i], recv_sem=recv.at[q, i],
+            device_id=(me, to), device_id_type=MESH,
+        )
+
+    def sends(q):
+        other = 1 - x
+        return {
+            0: (z, x, 0, strip, partner),
+            1: (z, x, 0, strip, above),
+            2: (z, x, 0, strip, below),
+            3: (z, other, 0, near, above),
+            4: (z, other, 0, near, below),
+            5: (down, x, near_half, near_half + far_half, above),
+            6: (up, x, 0, near_half, below),
+            7: (down, other, near_half, near_half, above),
+            8: (up, other, 0, near_half, below),
+            9: (up, x, tail, far_half, below),
+            10: (down, x, near, 2 * far_half, partner),
+            11: (up, x, near, 2 * far_half, partner),
+            12: (far, x, near, far_half, partner),
+            13: (far, x, tail, far_half, partner),
+        }
+
+    def arrivals(q):
+        other = 1 - x
+        return {
+            0: (z, other, 0, strip, partner),
+            1: (down, x, 0, strip, below),
+            2: (up, x, 0, strip, above),
+            3: (down, other, 0, near, below),
+            4: (up, other, 0, near, above),
+            5: (far, x, near_half, near_half + far_half, below),
+            6: (far, x, 0, near_half, above),
+            7: (far, other, near_half, near_half, below),
+            8: (far, other, 0, near_half, above),
+            9: (far, x, tail, far_half, above),
+            10: (down, other, near, 2 * far_half, partner),
+            11: (up, other, near, 2 * far_half, partner),
+            12: (far, other, near, far_half, partner),
+            13: (far, other, tail, far_half, partner),
+        }
+
+    def start(q, i):
+        push(q, i, *sends(q)[i]).start()
+
+    def take(q, i):
+        push(q, i, *arrivals(q)[i]).wait_recv()
+
+    def own(q):
+        for i in (0, 1, 2):
+            start(q, i)
+
+    def forward(q):
+        for got, gives in ((0, (3, 4)), (1, (5, 10)), (2, (6, 9, 11)), (3, (7,)), (4, (8,)), (5, (12,)), (9, (13,))):
+            take(q, got)
+            for i in gives:
+                start(q, i)
+
+    def finish(q):
+        for i in (6, 7, 8, 10, 11, 12, 13):
+            take(q, i)
+
+    mine = pltpu.make_async_copy(
+        strip_ref, rows.at[pl.ds(pl.multiple_of(k * strip, PIECE), strip)], local_sem.at[0]
+    )
+    mine.start()
+
+    def rhs_place(source):
+        return resid.at[:, pl.ds(pl.multiple_of(source * cabs_local, PIECE), cabs_local)]
+
+    keep = pltpu.make_async_copy(rhs_ref.at[k], rhs_place(k), local_sem.at[1])
+    keep.start()
+
+    barrier = pltpu.get_barrier_semaphore()
+    for step in range(1, cols):
+        pl.semaphore_signal(barrier, inc=1, device_id=(me, (k + step) % cols), device_id_type=MESH)
+    for step in range(1, chains):
+        pl.semaphore_signal(barrier, inc=1, device_id=((me + step) % chains, k), device_id_type=MESH)
+    pl.semaphore_wait(barrier, cols + chains - 2)
+    mine.wait()
+    own(0)
+
+    def rhs_copy(step, place):
+        to = (k + step) % cols
+        return pltpu.make_async_remote_copy(
+            src_ref=rhs_ref.at[to], dst_ref=rhs_place(place),
+            send_sem=rhs_send.at[step - 1], recv_sem=rhs_recv.at[step - 1],
+            device_id=(me, to), device_id_type=MESH,
+        )
+
+    for step in range(1, cols):
+        rhs_copy(step, k).start()
+
+    pl.when(me >= 1)(lambda: own(1))
+    forward(0)
+    pl.when(me >= 2)(lambda: own(2))
+    finish(0)
+
+    diag_column = pl.multiple_of(me * aux, BLOCK)
+
+    def diag(s, t, count=1):
+        return rows[pl.ds(s * BLOCK, BLOCK), pl.ds(pl.multiple_of(diag_column + t * BLOCK, BLOCK), count * BLOCK)]
+
+    row_id = lax.broadcasted_iota(jnp.int32, (BLOCK, BLOCK), 0)
+    col_id = lax.broadcasted_iota(jnp.int32, (BLOCK, BLOCK), 1)
+    for s in range(blocks):
+        on = row_id == col_id
+        inverse[s] = jnp.where(on, 1.0 / jnp.where(on, diag(s, s), 1.0), 0.0)
+
+    def double(level, carry):
+        low_row, low_col = row_id >> level, col_id >> level
+        pick = ((low_row >> 1) == (low_col >> 1)) & (low_row > low_col)
+        for s in range(blocks):
+            off = jnp.where(pick, diag(s, s), 0.0)
+            inverse[s] = inverse[s] - plain(inverse[s], plain(off, inverse[s]))
+        return carry
+
+    lax.fori_loop(0, BLOCK.bit_length() - 1, double, 0)
+
+    keep.wait()
+    for step in range(1, cols):
+        rhs_copy(step, (k + cols - step) % cols).wait_recv()
+
+    def chain_copy(section, step):
+        to = (section + step) % chains
+        return pltpu.make_async_remote_copy(
+            src_ref=out_ref, dst_ref=solved.at[section],
+            send_sem=chain_send.at[step - 1], recv_sem=chain_recv.at[section],
+            device_id=(to, k), device_id_type=MESH,
+        )
+
+    tall = aux // 3 if aux % (3 * BLOCK) == 0 else BLOCK
+    for q in range(1, chains):
+
+        def section(q=q):
+            forward(q)
+            if q + 2 < chains + 0:
+                pl.when(me >= q + 2)(lambda: own(q + 2))
+            finish(q)
+            chain_copy(q - 1, 1).wait_recv()
+            arrived = solved[q - 1].reshape(width, aux)
+            for m in range(aux // tall):
+                part = pl.ds(m * tall, tall)
+                change = times_t(arrived, rows[part, pl.ds((q - 1) * aux, aux)])
+                resid[:, :, part] = resid[:, :, part] - change.reshape(resid.shape[0], resid.shape[1], tall)
+
+        pl.when(me >= q)(section)
+
+    shape = (out_ref.shape[0], out_ref.shape[1], BLOCK)
+    for s in range(blocks):
+        part = pl.ds(s * BLOCK, BLOCK)
+        left = resid[:, :, part].reshape(width, BLOCK)
+        if s:
+            left = left - times_t(out_ref[:, :, : s * BLOCK].reshape(width, s * BLOCK), diag(s, 0, s))
+        out_ref[:, :, part] = times_t(left, inverse[s]).reshape(shape)
+
+    for section in range(chains - 1):
+
+        def tell(section=section):
+            for step in range(1, chains - section):
+                chain_copy(section, step).start()
+            for step in range(1, chains - section):
+                chain_copy(section, step).wait_send()
+
+        pl.when(me == section)(tell)
+
+    for step in range(1, cols):
+        rhs_copy(step, k).wait_send()
+    for q in range(chains):
+
+        def settle(q=q):
+            for i, what in sends(q).items():
+                push(q, i, *what).wait_send()
+
+        pl.when(me >= q)(settle)
+
+
+def gathered(chains, ring, factor, right_side, occ_order, cabs_order):
+    cols = 2 * ring
+    strip = factor.shape[0]
+    aux = right_side.shape[0]
+    occ_total, cabs_total = occ_order.shape[0], cabs_order.shape[0]
+    cabs_local, occ_local = cabs_total // cols, occ_total // cols
+    rhs = right_side.reshape(aux, cabs_local, occ_total).transpose(2, 1, 0)
+    rhs = jnp.take(rhs, occ_order, axis=0).reshape(cols, occ_local, cabs_local, aux)
+    dma = pltpu.SemaphoreType.DMA
+    found = pl.pallas_call(
+        functools.partial(kernel, chains, ring),
+        out_shape=jax.ShapeDtypeStruct((occ_local, cabs_total, aux), jnp.float32),
+        in_specs=[pl.BlockSpec(memory_space=pl.ANY)] * 2,
+        out_specs=pl.BlockSpec(memory_space=pltpu.VMEM),
+        scratch_shapes=[
+            pltpu.VMEM((aux, factor.shape[1]), jnp.float32),
+            pltpu.VMEM((occ_local, cabs_total, aux), jnp.float32),
+            pltpu.VMEM((chains - 1, occ_local, cabs_total, aux), jnp.float32),
+            pltpu.VMEM((aux // BLOCK, BLOCK, BLOCK), jnp.float32),
+            dma((chains, 14)),
+            dma((chains, 14)),
+            dma((chains - 1,)),
+            dma((chains - 1,)),
+            dma((cols - 1,)),
+            dma((cols - 1,)),
+            dma((2,)),
+        ],
+        compiler_params=pltpu.CompilerParams(
+            collective_id=0, has_side_effects=True, vmem_limit_bytes=56 * 1024 * 1024
+        ),
+    )(factor, rhs)
+    return jnp.take(found, cabs_order, axis=1)
+
+
 def solution(mesh):
+    chains, cols = mesh.shape["chain"], mesh.shape["cols"]
+
+    def per_device(factor, right_side, occ_order, cabs_order):
+        tiled = factor.shape[0] % PIECE == 0 and right_side.shape[0] % BLOCK == 0
+        if tiled and cols // 2 == 4 and (cabs_order.shape[0] // cols) % PIECE == 0:
+            return gathered(chains, cols // 2, factor, right_side, occ_order, cabs_order)
+        return general(factor, right_side, occ_order, cabs_order)
+
     in_specs = (P(("chain", "cols"), None), P("chain", "cols"), P(), P())
     out_specs = P("cols", None, "chain")
     return jax.shard_map(

time: 743 us -> 275 us (0.37)
  waiting for transfers between devices: 529 us -> 0 us
  Pallas kernels: 0 us -> 263 us
  other arithmetic: 101 us -> 1.94 us
  matrix products: 55.8 us -> 0 us
  local copies, waits for them, and re-layouts: 32.7 us -> 5.77 us
  between operations: 13.9 us -> 0.09 us
    all_gather x1 -> x0, waiting for transfers between devices: 406 us -> none  [per_device(): factor_row = lax.all_gather(factor, 'cols', axis=0, tiled=True)]
    pallas_call x0 -> x1, Pallas kernels: none -> 263 us  [gathered(): pl.pallas_call(functools.partial(kernel, chains, ring), out_shape=jax.Sha...]
    psum x3 -> x0, waiting for transfers between devices: 114 us -> none  [from_root(): return lax.psum(kept, axis)]
    another operation x3 -> x0, other arithmetic: 94.1 us -> none  [per_device(): jax.scipy.linalg.solve_triangular(diag_block, identity, lower=True)]
    another operation x17 -> x0, matrix products: 29.2 us -> none  [per_device(): jax.scipy.linalg.solve_triangular(diag_block, identity, lower=True)]
    another operation x31 -> x0, local copies, waits for them, and re-layouts: 25.2 us -> none
    dot_general x3 -> x0, matrix products: 19.2 us -> none  [product(): jnp.dot(left, right, precision=lax.Precision.HIGHEST, preferred_element_t...]
    all_to_all x1 -> x0, waiting for transfers between devices: 9.83 us -> none  [per_device(): lax.all_to_all(grid, 'cols', split_axis=0, concat_axis=2, tiled=True)]
  transfers between devices with their start and end apart: 5 -> 0, of which waited for: 5 -> 0; matrix products, arithmetic and copies ran while one was open for 1% -> 0% of each run, Pallas kernels for 0% -> 0%
where the time goes in v1:
time: 275 us; the launch traced here: 271 us
  Pallas kernels  263 us (96%)
  local copies, waits for them, and re-layouts  5.77 us (2%)
    pallas_call x1, Pallas kernels, gathered(): pl.pallas_call(functools.partial(kernel, chains, ring), out_shape=jax.Sha...  263 us

profile of v1, /device:TPU:5, one launch (start us, length us, event | category | flops | bytes accessed | tf_op | source)
XLA Modules:
  0.0 270.9 jit_solution(9449770514255237159)
XLA Ops:
  0.0 0.0 copy-start
  0.0 1.3 copy.5
  1.3 0.2 copy.10
  1.5 0.7 compare_select_fusion
  2.2 0.6 gather_fusion
  2.8 0.0 copy-done
  2.8 0.1 broadcast_in_dim.27
  2.9 0.9 broadcast_select_fusion.rhs_ref
  3.8 0.0 copy-start.1
  3.8 263.1 %shard_map.46 = f32[2,64,1152]{2,1,0:T(8,128)} custom-call(f32[144,4608]{1,0:T(8,128)} %strip_ref.1, f32[8,2,8,1152]{3,2,1,0:T(8,128)} %broadcast_select_fusion.rhs_ref), custom_call_target="tpu_custom_call" | custom-call | tf_op jit(solution)/shard_map/pallas_call | solution.py:304
  267.0 1.5 copy.7
  268.5 0.0 copy-done.1
  268.5 1.2 gather_fusion.1
  269.8 0.3 select_bitcast_fusion
  270.1 0.9 copy.8
  (5 shorter events, 0.0 us)
Async XLA Ops:
  0.0 2.8 %copy-start = (s32[16]{0:T(128)S(1)}, s32[16]{0:T(128)}, u32[]{:S(2)}) copy-start(s32[16]{0:T(128)} %param.6) | copy-start | bytes 196
  3.8 264.7 %copy-start.1 = (s32[64]{0:T(128)S(1)}, s32[64]{0:T(128)}, u32[]{:S(2)}) copy-start(s32[64]{0:T(128)} %param.7) | copy-start | bytes 772

commit v2 on v1

v2 whole, which is shorter than its diff:
```python
import functools

import jax
import jax.numpy as jnp
from jax import lax
from jax.experimental import pallas as pl
from jax.experimental.pallas import tpu as pltpu
from jax.sharding import PartitionSpec as P

BLOCK = 128
PIECE = 8
MESH = pl.DeviceIdType.MESH


def from_root(value, axis, source):
    kept = jnp.where(lax.axis_index(axis) == source, value, 0).astype(value.dtype)
    return lax.psum(kept, axis)


def product(left, right):
    return jnp.dot(left, right, precision=lax.Precision.HIGHEST, preferred_element_type=jnp.float32)


def general(factor, right_side, occ_order, cabs_order):
    chain_size = lax.axis_size("chain")
    position = lax.axis_index("chain")
    factor_row = lax.all_gather(factor, "cols", axis=0, tiled=True)
    aux_rows = factor_row.shape[0]
    diag_block = lax.dynamic_slice_in_dim(factor_row, position * aux_rows, aux_rows, 1)
    identity = jnp.eye(aux_rows, dtype=jnp.float32)
    inverse = jax.scipy.linalg.solve_triangular(diag_block, identity, lower=True)

    def settle(residual):
        return product(inverse, residual)

    def blank(residual):
        return jnp.zeros_like(residual)

    residual = right_side
    solution = jnp.zeros_like(right_side)
    for section in range(chain_size):
        solved = lax.cond(position == section, settle, blank, residual)
        solution = solution + solved
        if section + 1 < chain_size:
            arrived = from_root(solved, "chain", section)
            coupling = factor_row[:, section * aux_rows : (section + 1) * aux_rows]

            def lower_block(current, arrived=arrived, coupling=coupling):
                return current - product(coupling, arrived)

            def keep_block(current):
                return current

            residual = lax.cond(position > section, lower_block, keep_block, residual)
    occ_total = occ_order.shape[0]
    cabs_local = right_side.shape[1] // occ_total
    cols_size = lax.axis_size("cols")
    occ_local = occ_total // cols_size
    grid = solution.reshape(aux_rows, cabs_local, occ_total)
    grid = jnp.take(grid, occ_order, axis=2)
    grid = grid.reshape(aux_rows, cabs_local, cols_size, occ_local)
    grid = jnp.transpose(grid, (2, 3, 1, 0))
    moved = jnp.take(
        lax.all_to_all(grid, "cols", split_axis=0, concat_axis=2, tiled=True), cabs_order, axis=2
    )
    return moved.reshape(occ_local, moved.shape[2], aux_rows)


def times_t(left, right, exact=False):
    precision = lax.Precision.HIGHEST
    dims = (((1,), (1,)), ((), ()))
    if exact:
        return lax.dot_general(left, right, dims, precision=precision, preferred_element_type=jnp.float32)
    left_hi = left.astype(jnp.bfloat16)
    left_lo = (left - left_hi.astype(jnp.float32)).astype(jnp.bfloat16)
    right_hi = right.astype(jnp.bfloat16)
    right_lo = (right - right_hi.astype(jnp.float32)).astype(jnp.bfloat16)
    dot = functools.partial(lax.dot_general, dimension_numbers=dims, preferred_element_type=jnp.float32)
    return dot(left_hi, right_hi) + (dot(left_hi, right_lo) + dot(left_lo, right_hi))


def plain(left, right):
    return jnp.dot(left, right, precision=lax.Precision.HIGHEST, preferred_element_type=jnp.float32)


def kernel(
    chains, ring, strip_ref, rhs_ref, out_ref, rows, resid, solved, found, inverse,
    up_send, down_send, line_recv, side_up_send, side_down_send, side_recv, cross_send, cross_recv,
    swap_send, swap_recv, chain_send, chain_recv, rhs_send, rhs_recv, out_sem, local_sem,
):
    cols = 2 * ring
    strip = strip_ref.shape[0]
    aux = strip * cols
    blocks = aux // BLOCK
    cabs_local = rhs_ref.shape[2]
    width = found.shape[0] * found.shape[1]
    me = lax.axis_index("chain")
    k = lax.axis_index("cols")
    z = k // 2
    x = k % 2
    partner = 2 * z + (1 - x)
    odd = me % 2
    even = me % 2 == 0
    peer = me + odd * (chains - 2 * me)
    role = peer

    def place_of(job):
        return job + (job % 2) * (chains - 2 * job)

    units = strip // PIECE
    side = (units + 3) // 6 * PIECE
    early = ((ring // 2 * 2 * strip + BLOCK - 1) // BLOCK) * BLOCK
    pieces = [(0, 0, early, 0), (0, early, aux - early, ring // 2)]
    pieces += [(q, 0, aux, 0) for q in range(1, chains)]

    def columns(p, job):
        q, begin, count, _ = pieces[p]
        start = job * aux if q == 0 else (q - 1) * aux
        return pl.ds(pl.multiple_of(start + begin, BLOCK), count)

    def slot(p, zz, xx, begin, size):
        start = pl.multiple_of((2 * zz + xx) * strip + begin, PIECE)
        return rows.at[pl.ds(start, size), columns(p, role)]

    def push(p, zz, xx, begin, size, send, recv, to):
        ref = slot(p, zz, xx, begin, size)
        return pltpu.make_async_remote_copy(
            src_ref=ref, dst_ref=ref, send_sem=send.at[p, zz], recv_sem=recv.at[p, zz],
            device_id=(me, to), device_id_type=MESH,
        )

    def line(p, zz, upward):
        send = up_send if upward else down_send
        return push(p, zz, x, 0, strip, send, line_recv, 2 * (z + 1 if upward else z - 1) + x)

    def aside(p, zz, upward):
        send = side_up_send if upward else side_down_send
        return push(p, zz, 1 - x, 0, side, send, side_recv, 2 * (z + 1 if upward else z - 1) + x)

    def cross(p, zz, xx, whole):
        begin = 0 if whole else side
        return push(p, zz, xx, begin, strip - begin, cross_send, cross_recv, partner)

    top = ring - 1

    def has(p, zz):
        return zz >= pieces[p][3]

    def own(p):
        @pl.when(has(p, z))
        def _():
            cross(p, z, x, True).start()
            pl.when(z < top)(lambda: line(p, z, True).start())
            pl.when(z > 0)(lambda: line(p, z, False).start())

    def from_below(p, d):
        return (z >= d) & has(p, z - d)

    def from_above(p, d):
        return (z + d <= top) & has(p, z + d)

    def forward(p, following):
        for d in range(1, ring):

            @pl.when(from_below(p, d))
            def _():
                line(p, z - d, True).wait_recv()
                pl.when(z < top)(lambda: line(p, z - d, True).start())
                cross(p, z - d, x, False).start()

            @pl.when(from_above(p, d))
            def _():
                line(p, z + d, False).wait_recv()
                pl.when(z > 0)(lambda: line(p, z + d, False).start())
                cross(p, z + d, x, False).start()

            if d == 1:

                @pl.when(has(p, z))
                def _():
                    cross(p, z, 1 - x, True).wait_recv()
                    pl.when(z < top)(lambda: aside(p, z, True).start())
                    pl.when(z > 0)(lambda: aside(p, z, False).start())

                following()

            @pl.when(from_below(p, d))
            def _():
                aside(p, z - d, True).wait_recv()
                pl.when(z < top)(lambda: aside(p, z - d, True).start())

            @pl.when(from_above(p, d))
            def _():
                aside(p, z + d, False).wait_recv()
                pl.when(z > 0)(lambda: aside(p, z + d, False).start())

    def finish(p):
        for d in range(1, ring):
            pl.when(from_below(p, d))(lambda: cross(p, z - d, 1 - x, False).wait_recv())
            pl.when(from_above(p, d))(lambda: cross(p, z + d, 1 - x, False).wait_recv())

    def settle(p):
        pl.when(has(p, z))(lambda: cross(p, z, x, True).wait_send())
        pl.when(has(p, z) & (z < top))(lambda: line(p, z, True).wait_send())
        pl.when(has(p, z) & (z > 0))(lambda: line(p, z, False).wait_send())
        pl.when(has(p, z) & (z < top))(lambda: aside(p, z, True).wait_send())
        pl.when(has(p, z) & (z > 0))(lambda: aside(p, z, False).wait_send())
        for d in range(1, ring):

            @pl.when(from_below(p, d))
            def _():
                cross(p, z - d, x, False).wait_send()

                @pl.when(z < top)
                def _():
                    line(p, z - d, True).wait_send()
                    aside(p, z - d, True).wait_send()

            @pl.when(from_above(p, d))
            def _():
                cross(p, z + d, x, False).wait_send()

                @pl.when(z > 0)
                def _():
                    line(p, z + d, False).wait_send()
                    aside(p, z + d, False).wait_send()

    mine = pl.ds(pl.multiple_of(k * strip, PIECE), strip)

    def load():
        return pltpu.make_async_copy(strip_ref, rows.at[mine], local_sem.at[0])

    def swap(p, job):
        return pltpu.make_async_remote_copy(
            src_ref=strip_ref.at[:, columns(p, job)], dst_ref=rows.at[mine, columns(p, job)],
            send_sem=swap_send.at[p], recv_sem=swap_recv.at[p],
            device_id=(peer, k), device_id_type=MESH,
        )

    def rhs_place(source):
        return resid.at[:, pl.ds(pl.multiple_of(source * cabs_local, PIECE), cabs_local)]

    def keep():
        return pltpu.make_async_copy(rhs_ref.at[k], rhs_place(k), local_sem.at[1])

    def rhs_copy(step, source):
        to = (k + step) % cols
        return pltpu.make_async_remote_copy(
            src_ref=rhs_ref.at[to], dst_ref=rhs_place(source),
            send_sem=rhs_send.at[step], recv_sem=rhs_recv.at[step],
            device_id=(peer, to), device_id_type=MESH,
        )

    @pl.when(even)
    def _():
        load().start()
        keep().start()

    barrier = pltpu.get_barrier_semaphore()
    for step in range(1, cols):
        pl.semaphore_signal(barrier, inc=1, device_id=(me, (k + step) % cols), device_id_type=MESH)
    for step in range(1, chains):
        pl.semaphore_signal(barrier, inc=1, device_id=((me + step) % chains, k), device_id_type=MESH)

    @pl.when(odd == 1)
    def _():
        for step in range(1, cols):
            pl.semaphore_signal(barrier, inc=1, device_id=(peer, (k + step) % cols), device_id_type=MESH)

    pl.semaphore_wait(barrier, cols + chains - 2 + odd * (cols - 1))

    @pl.when(odd == 1)
    def _():
        for p in range(len(pieces)):
            pl.when((me >= pieces[p][0]) & has(p, z))(lambda: swap(p, me).start())
        rhs_copy(0, k).start()

    def ready(p):
        pl.when((odd == 1) & has(p, z))(lambda: swap(p, role).wait_recv())
        own(p)

    pl.when(even)(lambda: load().wait())
    ready(0)
    for step in range(1, cols):
        rhs_copy(step, k).start()

    forward(0, lambda: ready(1))
    forward(1, lambda: pl.when(role >= 1)(lambda: ready(2)))
    finish(0)
    finish(1)

    diag_column = pl.multiple_of(role * aux, BLOCK)

    def diag(s, t, count=1):
        return rows[pl.ds(s * BLOCK, BLOCK), pl.ds(pl.multiple_of(diag_column + t * BLOCK, BLOCK), count * BLOCK)]

    row_id = lax.broadcasted_iota(jnp.int32, (BLOCK, BLOCK), 0)
    col_id = lax.broadcasted_iota(jnp.int32, (BLOCK, BLOCK), 1)
    for s in range(blocks):
        on = row_id == col_id
        inverse[s] = jnp.where(on, 1.0 / jnp.where(on, diag(s, s), 1.0), 0.0)

    def double(level, carry):
        low_row, low_col = row_id >> level, col_id >> level
        pick = ((low_row >> 1) == (low_col >> 1)) & (low_row > low_col)
        for s in range(blocks):
            off = jnp.where(pick, diag(s, s), 0.0)
            inverse[s] = inverse[s] - plain(inverse[s], plain(off, inverse[s]))
        return carry

    lax.fori_loop(0, BLOCK.bit_length() - 1, double, 0)

    pl.when(even)(lambda: keep().wait())
    pl.when(odd == 1)(lambda: rhs_copy(0, k).wait_recv())
    for step in range(1, cols):
        rhs_copy(step, (k + cols - step) % cols).wait_recv()

    def chain_copy(section, step):
        return pltpu.make_async_remote_copy(
            src_ref=found, dst_ref=solved.at[section],
            send_sem=chain_send.at[step - 1], recv_sem=chain_recv.at[section],
            device_id=(place_of((section + step) % chains), k), device_id_type=MESH,
        )

    tall = aux // 3 if aux % (3 * BLOCK) == 0 else BLOCK
    for q in range(1, chains):

        def section(q=q):
            p = q + 1
            following = (lambda: pl.when(role >= q + 1)(lambda: ready(p + 1))) if q + 1 < chains else (lambda: None)
            forward(p, following)
            finish(p)
            chain_copy(q - 1, 1).wait_recv()
            arrived = solved[q - 1].reshape(width, aux)
            for m in range(aux // tall):
                part = pl.ds(m * tall, tall)
                change = times_t(arrived, rows[part, pl.ds((q - 1) * aux, aux)])
                resid[:, :, part] = resid[:, :, part] - change.reshape(resid.shape[0], resid.shape[1], tall)

        pl.when(role >= q)(section)

    shape = (found.shape[0], found.shape[1], BLOCK)
    for s in range(blocks):
        part = pl.ds(s * BLOCK, BLOCK)
        left = resid[:, :, part].reshape(width, BLOCK)
        if s:
            left = left - times_t(found[:, :, : s * BLOCK].reshape(width, s * BLOCK), diag(s, 0, s))
        found[:, :, part] = times_t(left, inverse[s]).reshape(shape)

    def give():
        return pltpu.make_async_remote_copy(
            src_ref=found, dst_ref=out_ref, send_sem=out_sem.at[0], recv_sem=out_sem.at[1],
            device_id=(peer, k), device_id_type=MESH,
        )

    def put():
        return pltpu.make_async_copy(found, out_ref, local_sem.at[0])

    for section in range(chains - 1):

        def tell(section=section):
            for step in range(1, chains - section):
                chain_copy(section, step).start()
            for step in range(1, chains - section):
                chain_copy(section, step).wait_send()

        pl.when(role == section)(tell)

    pl.when(odd == 1)(lambda: give().start())
    pl.when(even)(lambda: put().start())
    for step in range(1, cols):
        rhs_copy(step, k).wait_send()
    for p in range(len(pieces)):
        pl.when(role >= pieces[p][0])(lambda: settle(p))

    @pl.when(odd == 1)
    def _():
        rhs_copy(0, k).wait_send()
        for p in range(len(pieces)):
            pl.when((me >= pieces[p][0]) & has(p, z))(lambda: swap(p, me).wait_send())
        give().wait_send()
        give().wait_recv()

    pl.when(even)(lambda: put().wait())


def gathered(chains, ring, factor, right_side, occ_order, cabs_order):
    cols = 2 * ring
    strip = factor.shape[0]
    aux = right_side.shape[0]
    occ_total, cabs_total = occ_order.shape[0], cabs_order.shape[0]
    cabs_local, occ_local = cabs_total // cols, occ_total // cols
    rhs = right_side.reshape(aux, cabs_local, occ_total).transpose(2, 1, 0)
    rhs = jnp.take(rhs, occ_order, axis=0).reshape(cols, occ_local, cabs_local, aux)
    dma = pltpu.SemaphoreType.DMA
    found = pl.pallas_call(
        functools.partial(kernel, chains, ring),
        out_shape=jax.ShapeDtypeStruct((occ_local, cabs_total, aux), jnp.float32),
        in_specs=[pl.BlockSpec(memory_space=pl.ANY)] * 2,
        out_specs=pl.BlockSpec(memory_space=pl.ANY),
        scratch_shapes=[
            pltpu.VMEM((aux, factor.shape[1]), jnp.float32),
            pltpu.VMEM((occ_local, cabs_total, aux), jnp.float32),
            pltpu.VMEM((chains - 1, occ_local, cabs_total, aux), jnp.float32),
            pltpu.VMEM((occ_local, cabs_total, aux), jnp.float32),
            pltpu.VMEM((aux // BLOCK, BLOCK, BLOCK), jnp.float32),
            *[dma((chains + 1, ring)) for _ in range(8)],
            dma((chains + 1,)),
            dma((chains + 1,)),
            dma((chains - 1,)),
            dma((chains - 1,)),
            dma((cols,)),
            dma((cols,)),
            dma((2,)),
            dma((2,)),
        ],
        compiler_params=pltpu.CompilerParams(
            collective_id=0, has_side_effects=True, vmem_limit_bytes=56 * 1024 * 1024
        ),
    )(factor, rhs)
    return jnp.take(found, cabs_order, axis=1)


def solution(mesh):
    chains, cols = mesh.shape["chain"], mesh.shape["cols"]

    def per_device(factor, right_side, occ_order, cabs_order):
        tiled = factor.shape[0] % PIECE == 0 and right_side.shape[0] % BLOCK == 0
        if tiled and cols // 2 == 4 and chains == 4 and (cabs_order.shape[0] // cols) % PIECE == 0:
            return gathered(chains, cols // 2, factor, right_side, occ_order, cabs_order)
        return general(factor, right_side, occ_order, cabs_order)

    in_specs = (P(("chain", "cols"), None), P("chain", "cols"), P(), P())
    out_specs = P("cols", None, "chain")
    return jax.shard_map(
        per_device, mesh=mesh, in_specs=in_specs, out_specs=out_specs, check_vma=False
    )
```

time: 275 us -> 195 us (0.71); the launches traced: 271 us -> 194 us
  Pallas kernels: 263 us -> 186 us
    pallas_call x1, Pallas kernels: 263 us -> 186 us  [gathered(): pl.pallas_call(functools.partial(kernel, chains, ring), out_shape=jax.Sha...]
where the time goes in v2:
time: 195 us; the launch traced here: 194 us
  Pallas kernels  186 us (95%)
  local copies, waits for them, and re-layouts  5.77 us (3%)
    pallas_call x1, Pallas kernels, gathered(): pl.pallas_call(functools.partial(kernel, chains, ring), out_shape=jax.Sha...  186 us

profile of v2, /device:TPU:5, one launch (start us, length us, event | category | flops | bytes accessed | tf_op | source)
XLA Modules:
  0.0 193.9 jit_solution(12285521466467211769)
XLA Ops:
  0.0 0.0 copy-start
  0.0 1.3 copy.5
  1.3 0.2 copy.10
  1.5 0.7 compare_select_fusion
  2.2 0.6 gather_fusion
  2.8 0.0 copy-done
  2.8 0.1 broadcast_in_dim.27
  2.9 0.9 broadcast_select_fusion.rhs_ref
  3.8 0.0 copy-start.1
  3.8 186.1 %shard_map.46 = f32[2,64,1152]{2,1,0:T(8,128)} custom-call(f32[144,4608]{1,0:T(8,128)} %strip_ref.1, f32[8,2,8,1152]{3,2,1,0:T(8,128)} %broadcast_select_fusion.rhs_ref), custom_call_target="tpu_custom_call" | custom-call | tf_op jit(solution)/shard_map/pallas_call | solution.py:396
  189.9 1.5 copy.7
  191.4 0.0 copy-done.1
  191.5 1.2 gather_fusion.1
  192.7 0.3 select_bitcast_fusion
  193.0 0.9 copy.8
  (5 shorter events, 0.0 us)
Async XLA Ops:
  0.0 2.8 %copy-start = (s32[16]{0:T(128)S(1)}, s32[16]{0:T(128)}, u32[]{:S(2)}) copy-start(s32[16]{0:T(128)} %param.6) | copy-start | bytes 196
  3.8 187.6 %copy-start.1 = (s32[64]{0:T(128)S(1)}, s32[64]{0:T(128)}, u32[]{:S(2)}) copy-start(s32[64]{0:T(128)} %param.7) | copy-start | bytes 772

commit v3 on v2

--- a/solution.py
+++ b/solution.py
@@ -9,6 +9,7 @@
 
 BLOCK = 128
 PIECE = 8
+AHEAD = 3
 MESH = pl.DeviceIdType.MESH
 
 
@@ -111,7 +112,8 @@
     side = (units + 3) // 6 * PIECE
     early = ((ring // 2 * 2 * strip + BLOCK - 1) // BLOCK) * BLOCK
     pieces = [(0, 0, early, 0), (0, early, aux - early, ring // 2)]
-    pieces += [(q, 0, aux, 0) for q in range(1, chains)]
+    for q in range(1, chains):
+        pieces += [(q, 0, early, 0), (q, early, aux - early, 0)]
 
     def columns(p, job):
         q, begin, count, _ = pieces[p]
@@ -159,40 +161,37 @@
     def from_above(p, d):
         return (z + d <= top) & has(p, z + d)
 
-    def forward(p, following):
-        for d in range(1, ring):
-
-            @pl.when(from_below(p, d))
+    def stage(p, d):
+
+        @pl.when(from_below(p, d))
+        def _():
+            line(p, z - d, True).wait_recv()
+            pl.when(z < top)(lambda: line(p, z - d, True).start())
+            cross(p, z - d, x, False).start()
+
+        @pl.when(from_above(p, d))
+        def _():
+            line(p, z + d, False).wait_recv()
+            pl.when(z > 0)(lambda: line(p, z + d, False).start())
+            cross(p, z + d, x, False).start()
+
+        if d == 1:
+
+            @pl.when(has(p, z))
             def _():
-                line(p, z - d, True).wait_recv()
-                pl.when(z < top)(lambda: line(p, z - d, True).start())
-                cross(p, z - d, x, False).start()
-
-            @pl.when(from_above(p, d))
-            def _():
-                line(p, z + d, False).wait_recv()
-                pl.when(z > 0)(lambda: line(p, z + d, False).start())
-                cross(p, z + d, x, False).start()
-
-            if d == 1:
-
-                @pl.when(has(p, z))
-                def _():
-                    cross(p, z, 1 - x, True).wait_recv()
-                    pl.when(z < top)(lambda: aside(p, z, True).start())
-                    pl.when(z > 0)(lambda: aside(p, z, False).start())
-
-                following()
-
-            @pl.when(from_below(p, d))
-            def _():
-                aside(p, z - d, True).wait_recv()
-                pl.when(z < top)(lambda: aside(p, z - d, True).start())
-
-            @pl.when(from_above(p, d))
-            def _():
-                aside(p, z + d, False).wait_recv()
-                pl.when(z > 0)(lambda: aside(p, z + d, False).start())
+                cross(p, z, 1 - x, True).wait_recv()
+                pl.when(z < top)(lambda: aside(p, z, True).start())
+                pl.when(z > 0)(lambda: aside(p, z, False).start())
+
+        @pl.when(from_below(p, d))
+        def _():
+            aside(p, z - d, True).wait_recv()
+            pl.when(z < top)(lambda: aside(p, z - d, True).start())
+
+        @pl.when(from_above(p, d))
+        def _():
+            aside(p, z + d, False).wait_recv()
+            pl.when(z > 0)(lambda: aside(p, z + d, False).start())
 
     def finish(p):
         for d in range(1, ring):
@@ -283,11 +282,8 @@
     ready(0)
     for step in range(1, cols):
         rhs_copy(step, k).start()
-
-    forward(0, lambda: ready(1))
-    forward(1, lambda: pl.when(role >= 1)(lambda: ready(2)))
-    finish(0)
-    finish(1)
+    for p in range(1, AHEAD):
+        pl.when(role >= pieces[p][0])(lambda: ready(p))
 
     diag_column = pl.multiple_of(role * aux, BLOCK)
 
@@ -296,10 +292,6 @@
 
     row_id = lax.broadcasted_iota(jnp.int32, (BLOCK, BLOCK), 0)
     col_id = lax.broadcasted_iota(jnp.int32, (BLOCK, BLOCK), 1)
-    for s in range(blocks):
-        on = row_id == col_id
-        inverse[s] = jnp.where(on, 1.0 / jnp.where(on, diag(s, s), 1.0), 0.0)
-
     def double(level, carry):
         low_row, low_col = row_id >> level, col_id >> level
         pick = ((low_row >> 1) == (low_col >> 1)) & (low_row > low_col)
@@ -308,13 +300,6 @@
             inverse[s] = inverse[s] - plain(inverse[s], plain(off, inverse[s]))
         return carry
 
-    lax.fori_loop(0, BLOCK.bit_length() - 1, double, 0)
-
-    pl.when(even)(lambda: keep().wait())
-    pl.when(odd == 1)(lambda: rhs_copy(0, k).wait_recv())
-    for step in range(1, cols):
-        rhs_copy(step, (k + cols - step) % cols).wait_recv()
-
     def chain_copy(section, step):
         return pltpu.make_async_remote_copy(
             src_ref=found, dst_ref=solved.at[section],
@@ -323,21 +308,45 @@
         )
 
     tall = aux // 3 if aux % (3 * BLOCK) == 0 else BLOCK
-    for q in range(1, chains):
-
-        def section(q=q):
-            p = q + 1
-            following = (lambda: pl.when(role >= q + 1)(lambda: ready(p + 1))) if q + 1 < chains else (lambda: None)
-            forward(p, following)
-            finish(p)
-            chain_copy(q - 1, 1).wait_recv()
-            arrived = solved[q - 1].reshape(width, aux)
-            for m in range(aux // tall):
-                part = pl.ds(m * tall, tall)
-                change = times_t(arrived, rows[part, pl.ds((q - 1) * aux, aux)])
-                resid[:, :, part] = resid[:, :, part] - change.reshape(resid.shape[0], resid.shape[1], tall)
-
-        pl.when(role >= q)(section)
+
+    def invert():
+        for s in range(blocks):
+            on = row_id == col_id
+            inverse[s] = jnp.where(on, 1.0 / jnp.where(on, diag(s, s), 1.0), 0.0)
+        lax.fori_loop(0, BLOCK.bit_length() - 1, double, 0)
+        pl.when(even)(lambda: keep().wait())
+        pl.when(odd == 1)(lambda: rhs_copy(0, k).wait_recv())
+        for step in range(1, cols):
+            rhs_copy(step, (k + cols - step) % cols).wait_recv()
+
+    def update(q):
+        chain_copy(q - 1, 1).wait_recv()
+        arrived = solved[q - 1].reshape(width, aux)
+        for m in range(aux // tall):
+            part = pl.ds(m * tall, tall)
+            change = times_t(arrived, rows[part, pl.ds((q - 1) * aux, aux)])
+            resid[:, :, part] = resid[:, :, part] - change.reshape(resid.shape[0], resid.shape[1], tall)
+
+    def consume(p):
+        finish(p)
+        if p == 1:
+            invert()
+        if p > 1 and pieces[p][1]:
+            update(pieces[p][0])
+
+    def present(p):
+        return role >= pieces[p][0]
+
+    for t in range(len(pieces) + ring - 1):
+        for d in range(1, ring):
+            p = t - d + 1
+            if 0 <= p < len(pieces):
+                pl.when(present(p))(lambda: stage(p, d))
+            if d == 1 and t + AHEAD < len(pieces):
+                pl.when(present(t + AHEAD))(lambda: ready(t + AHEAD))
+        if t >= ring - 1:
+            p = t - ring + 1
+            pl.when(present(p))(lambda: consume(p))
 
     shape = (found.shape[0], found.shape[1], BLOCK)
     for s in range(blocks):
@@ -404,9 +413,9 @@
             pltpu.VMEM((chains - 1, occ_local, cabs_total, aux), jnp.float32),
             pltpu.VMEM((occ_local, cabs_total, aux), jnp.float32),
             pltpu.VMEM((aux // BLOCK, BLOCK, BLOCK), jnp.float32),
-            *[dma((chains + 1, ring)) for _ in range(8)],
-            dma((chains + 1,)),
-            dma((chains + 1,)),
+            *[dma((2 * chains, ring)) for _ in range(8)],
+            dma((2 * chains,)),
+            dma((2 * chains,)),
             dma((chains - 1,)),
             dma((chains - 1,)),
             dma((cols,)),

time: 195 us -> 196 us (level)
  Pallas kernels: 186 us -> 188 us
where the time goes in v3:
time: 196 us; the launch traced here: 195 us
  Pallas kernels  188 us (96%)
  local copies, waits for them, and re-layouts  5.77 us (3%)
    pallas_call x1, Pallas kernels, gathered(): pl.pallas_call(functools.partial(kernel, chains, ring), out_shape=jax.Sha...  188 us

profile of v3, /device:TPU:5, one launch (start us, length us, event | category | flops | bytes accessed | tf_op | source)
XLA Modules:
  0.0 195.4 jit_solution(4308760479099966952)
XLA Ops:
  0.0 0.0 copy-start
  0.0 1.3 copy.5
  1.3 0.2 copy.10
  1.5 0.7 compare_select_fusion
  2.2 0.6 gather_fusion
  2.8 0.0 copy-done
  2.8 0.1 broadcast_in_dim.27
  2.9 0.9 broadcast_select_fusion.rhs_ref
  3.8 0.0 copy-start.1
  3.8 187.6 %shard_map.46 = f32[2,64,1152]{2,1,0:T(8,128)} custom-call(f32[144,4608]{1,0:T(8,128)} %strip_ref.1, f32[8,2,8,1152]{3,2,1,0:T(8,128)} %broadcast_select_fusion.rhs_ref), custom_call_target="tpu_custom_call" | custom-call | tf_op jit(solution)/shard_map/pallas_call | solution.py:405
  191.4 1.5 copy.7
  192.9 0.0 copy-done.1
  193.0 1.2 gather_fusion.1
  194.2 0.3 select_bitcast_fusion
  194.5 0.9 copy.8
  (5 shorter events, 0.0 us)
Async XLA Ops:
  0.0 2.8 %copy-start = (s32[16]{0:T(128)S(1)}, s32[16]{0:T(128)}, u32[]{:S(2)}) copy-start(s32[16]{0:T(128)} %param.6) | copy-start | bytes 196
  3.8 189.1 %copy-start.1 = (s32[64]{0:T(128)S(1)}, s32[64]{0:T(128)}, u32[]{:S(2)}) copy-start(s32[64]{0:T(128)} %param.7) | copy-start | bytes 772
